TPU v7x, 32 devices: a whole 2x2x4 slice. The times are simulated.
32 devices in a mesh: row: 4 (over y, x), col: 8 (over z, core).
Axes of the slice: x: 2, y: 2, z: 4, core: 2. Of those that a mesh axis runs over, the one named last changes fastest.
Arguments:
- charge: float32 [256, 256, 256], P('col', 'row'), may hold values from -6 to 6
- green_spectrum: float32 [512, 512, 512], P('row', 'col'), may hold values from 0.2 to 2
Outputs:
- potential: float32 [256, 256, 256], P('col', 'row')
All inputs are finite; a program needn't handle non-finite values.
Results may differ from a plain program's by a relative error of at most 0.00007.
Values sent between devices are 32-bit elements; how exact they have to be, the bound alone decides.
A program may use at most 192 MiB of HBM per device.

v0:
```python
import math
import jax
import jax.numpy as jnp
from jax import lax
from jax.sharding import PartitionSpec as P

M = 512
N = 256


def phases(count_in, count_out, length):
    row_ids = lax.iota(jnp.int32, count_in)[:, None]
    col_ids = lax.iota(jnp.int32, count_out)[None, :]
    turn_ids = row_ids * col_ids % length
    angles = turn_ids.astype(jnp.float32) * (2.0 * math.pi / length)
    return (jnp.cos(angles), jnp.sin(angles))


def forward_table(count_in, count_out, length):
    cosine, sine_part = phases(count_in, count_out, length)
    return jnp.stack([jnp.stack([cosine, -sine_part], 1), jnp.stack([sine_part, cosine], 1)], 0)


def inverse_table(count_in, count_out, length):
    cosine, sine_part = phases(count_in, count_out, length)
    scaling = 1.0 / length
    return (
        jnp.stack([jnp.stack([cosine, sine_part], 1), jnp.stack([-sine_part, cosine], 1)], 0)
        * scaling
    )


def contract(pattern, left_side, right_side):
    return jnp.einsum(
        pattern,
        left_side,
        right_side,
        precision=lax.Precision.HIGHEST,
        preferred_element_type=jnp.float32,
    )


def on_device(charge, green_spectrum):
    cosine, sine_part = phases(N, M, M)
    real_table = jnp.stack([cosine, -sine_part], 1)
    along_z = contract("xyz,zqk->xyqk", charge, real_table)
    by_rows = lax.all_to_all(along_z, "row", split_axis=3, concat_axis=1, tiled=True)
    forward = forward_table(N, M, M)
    along_y = contract("xypk,pyqb->xkqb", by_rows, forward)
    spectrum = contract(
        "xkpj,pxqa->kjqa",
        lax.all_to_all(along_y, "col", split_axis=3, concat_axis=0, tiled=True),
        forward,
    )
    product = spectrum * green_spectrum[:, :, None, :]
    back_table = inverse_table(M, N, M)
    back_cos, back_sin = phases(M, N, M)
    real_back = jnp.stack([back_cos, -back_sin], 0) * (1.0 / M)
    back_x = contract("kjqa,qapx->kjpx", product, back_table)
    by_cols = lax.all_to_all(back_x, "col", split_axis=3, concat_axis=1, tiled=True)
    back_y = contract("kbpx,pbqy->kxqy", by_cols, back_table)
    return contract(
        "cxpy,pcz->xyz",
        lax.all_to_all(back_y, "row", split_axis=3, concat_axis=0, tiled=True),
        real_back,
    )


def solution(mesh):
    in_specs = (P("col", "row", None), P("row", "col", None))
    out_specs = P("col", "row", None)
    return jax.shard_map(
        on_device, mesh=mesh, in_specs=in_specs, out_specs=out_specs, check_vma=False
    )
```

profile of v0, /device:TPU:0, one launch (start us, length us, event | category | flops | bytes accessed | tf_op | source)
XLA Modules:
  0.0 1348.2 jit_solution(13706535293127981104)
XLA Ops:
  0.0 0.0 copy-start
  0.0 2.1 fusion.58
  2.1 0.0 copy-done
  2.1 9.0 convolution_bitcast_fusion.1
  11.1 16.2 %copy.38 = f32[32,64,2,512]{1,0,2,3:T(8,128)} copy(f32[32,64,2,512]{3,1,0,2:T(8,128)} %convolution_bitcast_fusion.1) | data formatting | bytes 16777216 | tf_op jit(solution)/shard_map/xyz,zqk->xyqk/dot_general | solution.py:34
  27.3 14.3 %reshape.237 = f32[4,1,524288]{2,1,0:T(1,128)} reshape(f32[512,2,32,64]{3,2,1,0:T(8,128)} %bitcast.107) | data formatting | bytes 16777216
  41.7 5.8 all-to-all-start
  47.5 1.9 fusion.57
  49.4 0.3 fusion.34
  49.7 91.6 %all-to-all-done = f32[4,1,524288]{2,1,0:T(1,128)} async-done(((f32[4,1,524288]{2,1,0:T(1,128)}), f32[4,1,524288]{2,1,0:T(1,128)}, u32[]{:S(2)}, u32[]{:S(2)}) %all-to-all-start) | async-done | bytes 8388640 | tf_op jit(solution)/shard_map/all_to_all | solution.py:47
  141.4 0.5 broadcast.343
  141.9 28.2 %reduce = f32[4,524288]{1,0:T(4,128)} reduce(f32[4,1,524288]{2,1,0:T(1,128)} %all-to-all-done, f32[]{:T(128)} %broadcast.343), dimensions={1}, to_apply=%all_to_all.52.reduce_sub_computation | reduce | bytes 16777220 | tf_op jit(solution)/shard_map/all_to_all | solution.py:47
  170.1 16.8 %reshape.238 = f32[512,2,32,64]{3,2,1,0:T(8,128)} reshape(f32[4,524288]{1,0:T(4,128)} %reduce) | data formatting | bytes 16777216
  186.9 12.8 copy.67
  199.6 4.7 copy.40
  204.3 30.4 %convolution_bitcast_fusion = f32[32,128,2,512]{3,1,2,0:T(8,128)} fusion(f32[32,256,2,128,1]{3,1,2,4,0:T(8,128)S(1)} %bitcast.111, f32[1,256,2,512]{3,1,2,0:T(8,128)S(1)} %get-tuple-element.8, f32[1,256,2,512]{3,1,2,0:T(8,128)S(1)} %get-tuple-element.7), kind=kOutput, calls=%fused_computation.9 | convolution fusion | flops 25770328064 | bytes 27262976 | tf_op jit(solution)/shard_map/xypk,pyqb->xkqb/dot_general | solution.py:34
  234.7 25.1 %copy.43 = f32[32,128,2,512]{1,2,0,3:T(2,128)} copy(f32[32,128,2,512]{3,1,2,0:T(8,128)} %convolution_bitcast_fusion) | data formatting | bytes 33554432 | tf_op jit(solution)/shard_map/xypk,pyqb->xkqb/dot_general | solution.py:34
  259.8 5.9 all-to-all-start.1
  265.7 17.7 %copy.48 = f32[128,64,512]{2,0,1:T(8,128)} copy(f32[128,64,512]{2,1,0:T(8,128)} %param.3) | data formatting | bytes 33554432 | tf_op args[1]
  283.4 1.9 fusion.60
  285.3 2.1 fusion.55
  287.4 1.5 fusion.78
  288.9 1.1 maximum_bitcast_fusion.1
  290.0 339.3 %all-to-all-done.1 = f32[32,128,2,512]{1,2,0,3:T(2,128)} async-done(((f32[32,128,2,512]{1,2,0,3:T(2,128)}), f32[32,128,2,512]{1,2,0,3:T(2,128)}, u32[]{:S(2)}, u32[]{:S(2)}) %all-to-all-start.1) | async-done | bytes 16777248 | tf_op jit(solution)/shard_map/all_to_all | solution.py:52
  629.3 11.0 copy.44
  640.3 0.0 copy-start.2
  640.3 1.8 copy.45
  642.1 0.0 copy-done.2
  642.1 0.0 copy-start.3
  642.1 71.3 %fusion.4 = f32[128,64,2,512,1]{3,0,4,2,1:T(8,128)} fusion(f32[256,128,2,64,1]{1,3,2,0,4:T(8,128)S(1)} %bitcast.106, f32[2,256,2,512,1]{3,1,0,2,4:T(8,128)S(1)} %copy-done.2), kind=kOutput, calls=%fused_computation.5 | convolution fusion | flops 51539607552 | bytes 52428800 | tf_op jit(solution)/shard_map/xkpj,pxqa->kjqa/dot_general | solution.py:34
  713.5 0.0 copy-done.3
  713.5 58.4 %fusion.7 = f32[128,64,2,256]{3,0,2,1:T(8,128)} fusion(f32[128,64,2,512,1]{3,0,4,2,1:T(8,128)} %fusion.4, f32[128,64,512]{2,0,1:T(8,128)} %copy.48, f32[1,512,2,256]{3,1,0,2:T(8,128)S(1)} %copy-done.3, f32[1,512,2,256]{3,1,0,2:T(8,128)S(1)} %get-tuple-element.5), kind=kOutput, calls=%fused_computation.8 | convolution fusion | flops 51549044736 | bytes 69206016 | tf_op jit(solution)/shard_map/kjqa,qapx->kjpx/dot_general | solution.py:34
  771.9 25.0 %copy.50 = f32[128,64,2,256]{0,2,1,3:T(2,128)} copy(f32[128,64,2,256]{3,0,2,1:T(8,128)} %fusion.7) | data formatting | bytes 33554432 | tf_op jit(solution)/shard_map/kjqa,qapx->kjpx/dot_general | solution.py:34
  796.9 367.8 %all_to_all.72 = f32[128,64,2,256]{0,2,1,3:T(2,128)S(1)} all-to-all(f32[128,64,2,256]{0,2,1,3:T(2,128)} %copy.50), channel_id=1, replica_groups=mesh['row'=4,'col'=8] {'col'}, dimensions={3} | all-to-all | bytes 33554432 | tf_op jit(solution)/shard_map/all_to_all | solution.py:60
  1164.7 10.3 copy.51
  1175.0 0.0 copy-start.4
  1175.0 7.0 copy.52
  1182.0 0.0 copy-done.4
  1182.0 37.7 %fusion.13 = f32[128,32,2,256]{3,0,2,1:T(8,128)} fusion(f32[128,512,2,32,1]{0,3,2,1,4:T(8,128)} %bitcast.114, f32[1,512,2,256]{3,1,0,2:T(8,128)S(1)} %copy-done.4, f32[1,512,2,256]{3,1,0,2:T(8,128)S(1)} %get-tuple-element.5), kind=kOutput, calls=%fused_computation.13 | convolution fusion | flops 25770852352 | bytes 27262976 | tf_op jit(solution)/shard_map/kbpx,pbqy->kxqy/dot_general | solution.py:34
  1219.6 13.2 copy.54
  1232.9 5.9 all-to-all-start.3
  1238.7 2.1 sine_negate_fusion
  1240.8 90.0 %all-to-all-done.3 = f32[128,32,2,256]{0,2,1,3:T(2,128)} async-done(((f32[128,32,2,256]{0,2,1,3:T(2,128)}), f32[128,32,2,256]{0,2,1,3:T(2,128)}, u32[]{:S(2)}, u32[]{:S(2)}) %all-to-all-start.3) | async-done | bytes 8388640 | tf_op jit(solution)/shard_map/all_to_all | solution.py:64
  1330.8 0.0 copy-start.1
  1330.8 8.4 copy.55
  1339.2 8.5 fusion.22
  1347.7 0.0 copy-done.1
Async XLA Ops:
  0.0 2.1 copy-start
  41.7 99.7 %all-to-all-start = ((f32[4,1,524288]{2,1,0:T(1,128)}), f32[4,1,524288]{2,1,0:T(1,128)}, u32[]{:S(2)}, u32[]{:S(2)}) async-start(f32[4,1,524288]{2,1,0:T(1,128)} %reshape.237), calls=%async_computation | async-start | bytes 16777216 | tf_op jit(solution)/shard_map/all_to_all | solution.py:47
  259.8 369.5 %all-to-all-start.1 = ((f32[32,128,2,512]{1,2,0,3:T(2,128)}), f32[32,128,2,512]{1,2,0,3:T(2,128)}, u32[]{:S(2)}, u32[]{:S(2)}) async-start(f32[32,128,2,512]{1,2,0,3:T(2,128)} %copy.43), calls=%async_computation.1 | async-start | bytes 33554432 | tf_op jit(solution)/shard_map/all_to_all | solution.py:52
  640.3 1.8 copy-start.2
  642.1 71.4 %copy-start.3 = (f32[1,512,2,256]{3,1,0,2:T(8,128)S(1)}, f32[1,512,2,256]{3,1,0,2:T(8,128)}, u32[]{:S(2)}) copy-start(f32[1,512,2,256]{3,1,0,2:T(8,128)} %get-tuple-element.6) | copy-start | bytes 3145732
  1175.0 7.0 copy-start.4
  1232.9 97.9 %all-to-all-start.3 = ((f32[128,32,2,256]{0,2,1,3:T(2,128)}), f32[128,32,2,256]{0,2,1,3:T(2,128)}, u32[]{:S(2)}, u32[]{:S(2)}) async-start(f32[128,32,2,256]{0,2,1,3:T(2,128)} %copy.54), calls=%async_computation.3 | async-start | bytes 16777216 | tf_op jit(solution)/shard_map/all_to_all | solution.py:64
  1330.8 16.9 %copy-start.1 = (f32[32,64,256]{2,1,0:T(8,128)S(1)}, f32[32,64,256]{2,1,0:T(8,128)}, u32[]{:S(2)}) copy-start(f32[32,64,256]{2,1,0:T(8,128)} %param.2) | copy-start | bytes 6291460
where the time goes:
time: 1360 us; the launch traced here: 1350 us
  waiting for transfers between devices  521 us (38%)
  blocking collectives  368 us (27%)
  matrix products  215 us (16%)
  local copies, waits for them, and re-layouts  185 us (14%)
  other arithmetic  41.2 us (3%)
  starting transfers between devices  17.6 us (1%)
    all_to_all x1, blocking collectives, on_device(): lax.all_to_all(back_x, 'col', split_axis=3, concat_axis=1, tiled=True)  368 us
    all_to_all x1, waiting for transfers between devices, on_device(): lax.all_to_all(along_y, 'col', split_axis=3, concat_axis=0, tiled=True)  339 us
    dot_general x6, matrix products, contract(): jnp.einsum(pattern, left_side, right_side, precision=lax.Precision.HIGHES...  215 us
    all_to_all x1, waiting for transfers between devices, on_device(): lax.all_to_all(along_z, 'row', split_axis=3, concat_axis=1, tiled=True)  91.6 us
    all_to_all x1, waiting for transfers between devices, on_device(): lax.all_to_all(back_y, 'row', split_axis=3, concat_axis=0, tiled=True)  90 us
    dot_general x4, local copies, waits for them, and re-layouts, contract(): jnp.einsum(pattern, left_side, right_side, precision=lax.Precision.HIGHES...  79.6 us
    unnamed x13, local copies, waits for them, and re-layouts  48.9 us
    all_to_all x1, other arithmetic, on_device(): lax.all_to_all(along_z, 'row', split_axis=3, concat_axis=1, tiled=True)  28.2 us
  transfers between devices with their start and end apart: 3, of which 3 were waited for; matrix products, arithmetic and copies ran while one was open for 2% of the time, Pallas kernels for 0%

commit v1 on v0

--- a/solution.py
+++ b/solution.py
@@ -6,6 +6,17 @@
 
 M = 512
 N = 256
+
+
+def in_blocks(value, dim, size):
+    before, after = (value.shape[:dim], value.shape[dim + 1 :])
+    return jnp.moveaxis(value.reshape(*before, size, -1, *after), dim, 0)
+
+
+def joined_along(pieces, dim):
+    dims = list(pieces.shape[1:])
+    dims[dim] *= pieces.shape[0]
+    return jnp.moveaxis(pieces, 0, dim).reshape(dims)
 
 
 def phases(count_in, count_out, length):
@@ -44,7 +55,14 @@
     cosine, sine_part = phases(N, M, M)
     real_table = jnp.stack([cosine, -sine_part], 1)
     along_z = contract("xyz,zqk->xyqk", charge, real_table)
-    by_rows = lax.all_to_all(along_z, "row", split_axis=3, concat_axis=1, tiled=True)
+    count, position = (lax.axis_size("row"), lax.axis_index("row"))
+    tiles = in_blocks(along_z, 3, count)
+    outs = [tiles[position]]
+    for step in range(1, count):
+        sent = tiles[position ^ step]
+        outs.append(lax.ppermute(sent, "row", [(i, i ^ step) for i in range(count)]))
+    tiles = jnp.stack(outs)[position ^ jnp.arange(count)]
+    by_rows = joined_along(tiles, 1)
     forward = forward_table(N, M, M)
     along_y = contract("xypk,pyqb->xkqb", by_rows, forward)
     spectrum = contract(

time: 1360 us -> 1310 us (0.963)
  other arithmetic: 41.2 us -> 16.6 us
  local copies, waits for them, and re-layouts: 185 us -> 161 us
    all_to_all x1 -> x0, waiting for transfers between devices: 91.6 us -> none  [on_device(): lax.all_to_all(along_z, 'row', split_axis=3, concat_axis=1, tiled=True)]
    ppermute x0 -> x3, waiting for transfers between devices: none -> 87.5 us  [on_device(): lax.ppermute(sent, 'row', [(i, i ^ step) for i in range(count)])]
    unnamed x13 -> x11, local copies, waits for them, and re-layouts: 48.9 us -> 17.8 us
    all_to_all x1 -> x0, other arithmetic: 28.2 us -> none  [on_device(): lax.all_to_all(along_z, 'row', split_axis=3, concat_axis=1, tiled=True)]
    another operation x0 -> x5, local copies, waits for them, and re-layouts: none -> 19.8 us
    all_to_all x3 -> x0, local copies, waits for them, and re-layouts: 18 us -> none  [on_device(): lax.all_to_all(along_z, 'row', split_axis=3, concat_axis=1, tiled=True)]
    dot_general x4 -> x3, local copies, waits for them, and re-layouts: 79.6 us -> 63.3 us  [contract(): jnp.einsum(pattern, left_side, right_side, precision=lax.Precision.HIGHES...]
  transfers between devices with their start and end apart: 3 -> 5, of which waited for: 3 -> 4; matrix products, arithmetic and copies ran while one was open for 2% -> 2% of each run, Pallas kernels for 0% -> 0%
where the time goes in v1:
time: 1310 us; the launch traced here: 1290 us
  waiting for transfers between devices  517 us (39%)
  blocking collectives  368 us (28%)
  matrix products  216 us (16%)
  local copies, waits for them, and re-layouts  161 us (12%)
  other arithmetic  16.6 us (1%)
  starting transfers between devices  16.5 us (1%)
    all_to_all x1, blocking collectives, on_device(): lax.all_to_all(back_x, 'col', split_axis=3, concat_axis=1, tiled=True)  368 us
    all_to_all x1, waiting for transfers between devices, on_device(): lax.all_to_all(along_y, 'col', split_axis=3, concat_axis=0, tiled=True)  339 us
    dot_general x6, matrix products, contract(): jnp.einsum(pattern, left_side, right_side, precision=lax.Precision.HIGHES...  216 us
    all_to_all x1, waiting for transfers between devices, on_device(): lax.all_to_all(back_y, 'row', split_axis=3, concat_axis=0, tiled=True)  90 us
    ppermute x3, waiting for transfers between devices, on_device(): lax.ppermute(sent, 'row', [(i, i ^ step) for i in range(count)])  87.5 us
    dot_general x3, local copies, waits for them, and re-layouts, contract(): jnp.einsum(pattern, left_side, right_side, precision=lax.Precision.HIGHES...  63.3 us
  transfers between devices with their start and end apart: 5, of which 4 were waited for; matrix products, arithmetic and copies ran while one was open for 2% of the time, Pallas kernels for 0%

profile of v1, /device:TPU:0, one launch (start us, length us, event | category | flops | bytes accessed | tf_op | source)
XLA Modules:
  0.0 1294.9 jit_solution(15800418459900412227)
XLA Ops:
  0.0 0.0 copy-start
  0.0 2.1 fusion.58
  2.1 9.0 convolution_bitcast_fusion.1
  11.1 9.9 reshape.251
  21.0 19.2 %constant_dynamic-slice_fusion.3 = (f32[32,64,2,1,128]{4,3,1,0,2:T(1,128)S(1)}, f32[32,64,2,1,128]{4,3,1,0,2:T(1,128)S(1)}, f32[32,64,2,1,128]{4,3,1,0,2:T(1,128)S(1)}, f32[32,64,2,1,128]{4,3,1,0,2:T(1,128)S(1)}) fusion(f32[32,64,2,4,128]{4,3,1,0,2:T(4,128)} %reshape.251, s32[]{:T(128)S(6)} %select_n.97, s32[]{:T(128)S(6)} %select_n.100, s32[]{:T(128)S(6)} %select_n.99, ...), kind=kLoop, calls=%fused_computation.83 | loop fusion | bytes 16777232 | tf_op jit(solution)/shard_map/dynamic-slice
  40.2 0.1 copy.90
  40.4 4.0 collective-permute-start.2
  44.4 0.1 copy.92
  44.5 0.6 collective-permute-start
  45.1 0.1 copy.91
  45.2 0.1 collective-permute-start.1
  45.4 0.1 copy.93
  45.5 1.9 fusion.57
  47.4 0.3 fusion.34
  47.7 43.1 %collective-permute-done.2 = f32[32,64,2,128]{3,1,2,0:T(8,128)S(1)} collective-permute-done((f32[32,64,2,128]{3,1,2,0:T(8,128)S(1)}, f32[32,64,2,128]{3,1,2,0:T(8,128)S(1)}, u32[]{:S(2)}, u32[]{:S(2)}) %collective-permute-start.2) | collective-permute-done | bytes 2097184 | tf_op jit(solution)/shard_map/ppermute | solution.py:63
  90.9 44.3 %collective-permute-done = f32[32,64,2,128]{3,1,2,0:T(8,128)S(1)} collective-permute-done((f32[32,64,2,128]{3,1,2,0:T(8,128)S(1)}, f32[32,64,2,128]{3,1,2,0:T(8,128)S(1)}, u32[]{:S(2)}, u32[]{:S(2)}) %collective-permute-start) | collective-permute-done | bytes 2097184 | tf_op jit(solution)/shard_map/ppermute | solution.py:63
  135.2 0.0 collective-permute-done.1
  135.2 3.6 pad_maximum_fusion
  138.9 7.7 gather_fusion
  146.6 4.2 copy.28
  150.8 30.5 %convolution_bitcast_fusion = f32[32,128,2,512]{3,1,2,0:T(8,128)} fusion(f32[32,256,2,128,1]{3,1,2,4,0:T(8,128)S(1)} %bitcast.127, f32[1,256,2,512]{3,1,2,0:T(8,128)S(1)} %get-tuple-element.12, f32[1,256,2,512]{3,1,2,0:T(8,128)S(1)} %get-tuple-element.11), kind=kOutput, calls=%fused_computation.10 | convolution fusion | flops 25770328064 | bytes 27262976 | tf_op jit(solution)/shard_map/xypk,pyqb->xkqb/dot_general | solution.py:45
  181.3 25.1 %copy.31 = f32[32,128,2,512]{1,2,0,3:T(2,128)} copy(f32[32,128,2,512]{3,1,2,0:T(8,128)} %convolution_bitcast_fusion) | data formatting | bytes 33554432 | tf_op jit(solution)/shard_map/xypk,pyqb->xkqb/dot_general | solution.py:45
  206.4 5.9 all-to-all-start
  212.3 17.7 %copy.36 = f32[128,64,512]{2,0,1:T(8,128)} copy(f32[128,64,512]{2,1,0:T(8,128)} %param.3) | data formatting | bytes 33554432 | tf_op args[1]
  230.0 1.9 fusion.60
  232.0 2.1 fusion.55
  234.0 1.5 fusion.79
  235.5 1.1 maximum_bitcast_fusion.1
  236.7 339.2 %all-to-all-done = f32[32,128,2,512]{1,2,0,3:T(2,128)} async-done(((f32[32,128,2,512]{1,2,0,3:T(2,128)}), f32[32,128,2,512]{1,2,0,3:T(2,128)}, u32[]{:S(2)}, u32[]{:S(2)}) %all-to-all-start) | async-done | bytes 16777248 | tf_op jit(solution)/shard_map/all_to_all | solution.py:70
  575.9 11.0 copy.32
  586.9 0.0 copy-start.2
  586.9 1.8 copy.33
  588.7 0.0 copy-done.2
  588.7 0.0 copy-start.3
  588.8 71.4 %fusion.4 = f32[128,64,2,512,1]{3,0,4,2,1:T(8,128)} fusion(f32[256,128,2,64,1]{1,3,2,0,4:T(8,128)S(1)} %bitcast.124, f32[2,256,2,512,1]{3,1,0,2,4:T(8,128)S(1)} %copy-done.2), kind=kOutput, calls=%fused_computation.6 | convolution fusion | flops 51539607552 | bytes 52428800 | tf_op jit(solution)/shard_map/xkpj,pxqa->kjqa/dot_general | solution.py:45
  660.1 58.5 %fusion.7 = f32[128,64,2,256]{3,0,2,1:T(8,128)} fusion(f32[128,64,2,512,1]{3,0,4,2,1:T(8,128)} %fusion.4, f32[128,64,512]{2,0,1:T(8,128)} %copy.36, f32[1,512,2,256]{3,1,0,2:T(8,128)S(1)} %copy-done.3, f32[1,512,2,256]{3,1,0,2:T(8,128)S(1)} %get-tuple-element.9), kind=kOutput, calls=%fused_computation.9 | convolution fusion | flops 51549044736 | bytes 69206016 | tf_op jit(solution)/shard_map/kjqa,qapx->kjpx/dot_general | solution.py:45
  718.6 25.0 %copy.38 = f32[128,64,2,256]{0,2,1,3:T(2,128)} copy(f32[128,64,2,256]{3,0,2,1:T(8,128)} %fusion.7) | data formatting | bytes 33554432 | tf_op jit(solution)/shard_map/kjqa,qapx->kjpx/dot_general | solution.py:45
  743.7 367.8 %all_to_all.54 = f32[128,64,2,256]{0,2,1,3:T(2,128)S(1)} all-to-all(f32[128,64,2,256]{0,2,1,3:T(2,128)} %copy.38), channel_id=1, replica_groups=mesh['row'=4,'col'=8] {'col'}, dimensions={3} | all-to-all | bytes 33554432 | tf_op jit(solution)/shard_map/all_to_all | solution.py:78
  1111.4 10.3 copy.39
  1121.7 7.0 copy.40
  1128.7 0.0 copy-done.4
  1128.7 37.7 %fusion.13 = f32[128,32,2,256]{3,0,2,1:T(8,128)} fusion(f32[128,512,2,32,1]{0,3,2,1,4:T(8,128)} %bitcast.130, f32[1,512,2,256]{3,1,0,2:T(8,128)S(1)} %copy-done.4, f32[1,512,2,256]{3,1,0,2:T(8,128)S(1)} %get-tuple-element.9), kind=kOutput, calls=%fused_computation.15 | convolution fusion | flops 25770852352 | bytes 27262976 | tf_op jit(solution)/shard_map/kbpx,pbqy->kxqy/dot_general | solution.py:45
  1166.4 13.2 %copy.42 = f32[128,32,2,256]{0,2,1,3:T(2,128)} copy(f32[128,32,2,256]{3,0,2,1:T(8,128)} %fusion.13) | data formatting | bytes 16777216 | tf_op jit(solution)/shard_map/kbpx,pbqy->kxqy/dot_general | solution.py:45
  1179.6 5.9 all-to-all-start.2
  1185.5 2.1 sine_negate_fusion
  1187.6 90.0 %all-to-all-done.2 = f32[128,32,2,256]{0,2,1,3:T(2,128)} async-done(((f32[128,32,2,256]{0,2,1,3:T(2,128)}), f32[128,32,2,256]{0,2,1,3:T(2,128)}, u32[]{:S(2)}, u32[]{:S(2)}) %all-to-all-start.2) | async-done | bytes 8388640 | tf_op jit(solution)/shard_map/all_to_all | solution.py:82
  1277.5 8.4 copy.43
  1285.9 8.5 fusion.22
  (7 shorter events, 0.0 us)
Async XLA Ops:
  0.0 2.1 copy-start
  40.4 50.5 %collective-permute-start.2 = (f32[32,64,2,128]{3,1,2,0:T(8,128)S(1)}, f32[32,64,2,128]{3,1,2,0:T(8,128)S(1)}, u32[]{:S(2)}, u32[]{:S(2)}) collective-permute-start(f32[32,64,2,128]{3,1,2,0:T(8,128)S(1)} %bitcast.132), channel_id=1, source_target_pairs={{0,24},{8,16},{16,8},{24,0},{1,25},{9,17},{17,9},{25,1},{2,26},{10... | collective-permute-start | bytes 6291464 | tf_op jit(solution)/shard_map/ppermute | solution.py:63
  44.5 90.7 %collective-permute-start = (f32[32,64,2,128]{3,1,2,0:T(8,128)S(1)}, f32[32,64,2,128]{3,1,2,0:T(8,128)S(1)}, u32[]{:S(2)}, u32[]{:S(2)}) collective-permute-start(f32[32,64,2,128]{3,1,2,0:T(8,128)S(1)} %bitcast.133), channel_id=1, source_target_pairs={{0,8},{8,0},{16,24},{24,16},{1,9},{9,1},{17,25},{25,17},{2,10},{10... | collective-permute-start | bytes 6291464 | tf_op jit(solution)/shard_map/ppermute | solution.py:63
  45.2 90.0 %collective-permute-start.1 = (f32[32,64,2,128]{3,1,2,0:T(8,128)S(1)}, f32[32,64,2,128]{3,1,2,0:T(8,128)S(1)}, u32[]{:S(2)}, u32[]{:S(2)}) collective-permute-start(f32[32,64,2,128]{3,1,2,0:T(8,128)S(1)} %bitcast.134), channel_id=1, source_target_pairs={{0,16},{8,24},{16,0},{24,8},{1,17},{9,25},{17,1},{25,9},{2,18},{10... | collective-permute-start | bytes 6291464 | tf_op jit(solution)/shard_map/ppermute | solution.py:63
  206.4 369.6 %all-to-all-start = ((f32[32,128,2,512]{1,2,0,3:T(2,128)}), f32[32,128,2,512]{1,2,0,3:T(2,128)}, u32[]{:S(2)}, u32[]{:S(2)}) async-start(f32[32,128,2,512]{1,2,0,3:T(2,128)} %copy.31), calls=%async_computation | async-start | bytes 33554432 | tf_op jit(solution)/shard_map/all_to_all | solution.py:70
  586.9 1.8 copy-start.2
  588.7 71.4 %copy-start.3 = (f32[1,512,2,256]{3,1,0,2:T(8,128)S(1)}, f32[1,512,2,256]{3,1,0,2:T(8,128)}, u32[]{:S(2)}) copy-start(f32[1,512,2,256]{3,1,0,2:T(8,128)} %get-tuple-element.10) | copy-start | bytes 3145732
  1121.7 7.0 copy-start.4
  1179.6 97.9 %all-to-all-start.2 = ((f32[128,32,2,256]{0,2,1,3:T(2,128)}), f32[128,32,2,256]{0,2,1,3:T(2,128)}, u32[]{:S(2)}, u32[]{:S(2)}) async-start(f32[128,32,2,256]{0,2,1,3:T(2,128)} %copy.42), calls=%async_computation.2 | async-start | bytes 16777216 | tf_op jit(solution)/shard_map/all_to_all | solution.py:82
  1277.5 16.9 %copy-start.1 = (f32[32,64,256]{2,1,0:T(8,128)S(1)}, f32[32,64,256]{2,1,0:T(8,128)}, u32[]{:S(2)}) copy-start(f32[32,64,256]{2,1,0:T(8,128)} %param.2) | copy-start | bytes 6291460
